TPU v7x, 32 devices: a whole 2x2x4 slice. The times are simulated.
32 devices in a mesh: tok: 4 (over z), out: 4 (over x, core), grp: 2 (over y).
Axes of the slice: x: 2, y: 2, z: 4, core: 2. Of those that a mesh axis runs over, the one named last changes fastest.
Arguments:
- activations: bfloat16 [1024, 2, 2048], P(('tok', 'grp'), None, 'out'), may hold values from -16 to 16
- out_grads: bfloat16 [1024, 2, 2048], P(('tok', 'grp'), None, 'out'), may hold values from -16 to 16
- weight: bfloat16 [2, 2048, 4096], P(None, 'out'), may hold values from -0.09375 to 0.09375
Outputs:
- update: bfloat16 [4096, 2, 2048], P(('tok', 'grp'), None, 'out')
- input_grad: bfloat16 [1024, 2, 2048], P(('tok', 'grp'), None, 'out')
All inputs are finite; a program needn't handle non-finite values.
Results may differ from a plain program's by a relative error of at most 0.0092.
Values may be sent and summed in bfloat16 or wider, within the bound.
A program may use at most 64 MiB of HBM per device.

v0:
```python
import math
import jax
import jax.numpy as jnp
from jax import lax
from jax.sharding import PartitionSpec as P

POWER = 3
DAMPING = 0.1
HIGH = lax.Precision.HIGHEST


def spread(piece):
    return lax.all_gather(piece, "out", axis=2, tiled=True)


def token_sums(maker, rows):
    return lax.psum_scatter(
        maker(jnp.int32(0), rows * lax.axis_size(("tok", "grp"))),
        ("tok", "grp"),
        scatter_dimension=0,
        tiled=True,
    )


def shared_rows(piece):
    return lax.all_gather(piece, ("tok", "grp"), axis=0, tiled=True)


def shared_total(vector):
    return lax.psum(vector, ("tok", "out", "grp"))


def diagonal_mask(rows, width, row_start, col_start):
    row_ids = row_start + lax.broadcasted_iota(jnp.int32, (rows, 1, width), 0)
    col_ids = col_start + lax.broadcasted_iota(jnp.int32, (rows, 1, width), 2)
    return jnp.where(row_ids == col_ids, 1.0, 0.0).astype(jnp.float32)


def multiply(left, right, gather_columns):
    row_band = spread(left)
    column_band = gather_columns(right)
    return jnp.einsum("rkj,jkc->rkc", row_band, column_band, preferred_element_type=jnp.float32)


def inverse_roots(tile, row_start, col_start, gather_columns, total):
    rows, count, width = tile.shape
    block = width * lax.axis_size("out")
    mask = diagonal_mask(rows, width, row_start, col_start)
    vector = jnp.ones((count, block), jnp.float32)
    image = vector
    for step in range(POWER):
        columns = lax.dynamic_slice_in_dim(vector, col_start, width, 1)
        part = jnp.einsum("rkc,kc->kr", tile, columns, precision=HIGH)
        placed = lax.dynamic_update_slice_in_dim(
            jnp.zeros((count, block), jnp.float32), part, row_start, 1
        )
        image = total(placed)
        if step + 1 < POWER:
            vector = image / jnp.sqrt(jnp.sum(image * image, axis=1, keepdims=True))
    scale = jnp.sum(vector * image, axis=1) / jnp.sum(vector * vector, axis=1)
    start = tile / scale[None, :, None]
    start_low = start.astype(jnp.bfloat16)
    first_low = ((3.0 * mask - start) / 2.0).astype(jnp.bfloat16)
    square_low = multiply(first_low, first_low, gather_columns).astype(jnp.bfloat16)
    moved = multiply(square_low, start_low, gather_columns)
    second_low = ((3.0 * mask - moved) / 2.0).astype(jnp.bfloat16)
    roots = multiply(first_low, second_low, gather_columns) / jnp.sqrt(scale)[None, :, None]
    return roots.astype(jnp.bfloat16)


def local(activations, out_grads, weight):
    tok_dev, blocks, width = activations.shape
    block = width * lax.axis_size("out")
    token_count = tok_dev * lax.axis_size("tok") * lax.axis_size("grp")
    col_start = lax.axis_index("out") * width
    local_sides = jnp.concatenate([activations, out_grads], axis=1)
    whole_sides = spread(local_sides)
    grads_whole = whole_sides[:, blocks:, :]
    weight_rows = weight.reshape(blocks, width, blocks, block)
    input_grad = jnp.einsum(
        "tjq,bcjq->tbc", grads_whole, weight_rows, preferred_element_type=jnp.float32
    ).astype(jnp.bfloat16)
    rows = block // (lax.axis_size("tok") * lax.axis_size("grp"))
    row_start = lax.axis_index(("tok", "grp")) * rows

    def shared_terms(start, span):
        return jnp.einsum(
            "tkr,tkc->rkc", whole_sides, local_sides, preferred_element_type=jnp.float32
        )

    sums = token_sums(shared_terms, rows)
    tile = sums / token_count + DAMPING * diagonal_mask(rows, width, row_start, col_start)
    roots = inverse_roots(tile, row_start, col_start, shared_rows, shared_total)
    bands = shared_rows(roots)
    whitened = jnp.einsum(
        "tkj,jkc->tkc", whole_sides, bands, preferred_element_type=jnp.float32
    ).astype(jnp.bfloat16)
    acts_whole = spread(whitened[:, :blocks, :]).reshape(tok_dev, blocks * block)
    grads_low = whitened[:, blocks:, :]
    owned_acts = lax.all_to_all(acts_whole, ("tok", "grp"), split_axis=1, concat_axis=0, tiled=True)
    update = jnp.einsum(
        "ta,tbc->abc",
        owned_acts,
        lax.all_gather(grads_low, ("tok", "grp"), axis=0, tiled=True),
        preferred_element_type=jnp.float32,
    )
    update = (update / math.sqrt(token_count)).astype(jnp.bfloat16)
    return (update, input_grad)


def token_space_whiten(sides, cols):
    tokens, block = sides.shape
    gram = jnp.einsum("tc,uc->tu", sides, sides, preferred_element_type=jnp.float32) / tokens
    ray_0 = jnp.sum(sides.astype(jnp.float32), axis=1)
    ray_1 = jnp.sum(gram * ray_0[None, :], axis=1) + DAMPING * ray_0
    ray_2 = jnp.sum(gram * ray_1[None, :], axis=1) + DAMPING * ray_1
    dots = [
        jnp.sum(ray_0 * ray_0),
        jnp.sum(ray_0 * ray_1),
        jnp.sum(ray_1 * ray_1),
        jnp.sum(ray_1 * ray_2),
        jnp.sum(ray_2 * ray_2),
    ]

    def moment(power):
        total = DAMPING**power * block
        for i in range(power):
            total = total + DAMPING ** (power - 1 - i) * dots[i] / tokens
        return total

    scale = moment(2 * POWER - 1) / moment(2 * POWER - 2)
    low = (gram / scale).astype(jnp.bfloat16)
    shift = DAMPING / scale

    def apply(value):
        product = jnp.einsum(
            "tu,uc->tc", low, value.astype(jnp.bfloat16), preferred_element_type=jnp.float32
        )
        return product + shift * value

    def first(value):
        return (3.0 * value - apply(value)) / 2.0

    head = first(cols.astype(jnp.float32))
    tail = first(first(apply(head)))
    return ((3.0 * head - tail) / 2.0 / jnp.sqrt(scale)).astype(jnp.bfloat16)


def planes(activations, out_grads, weight):
    tok_dev, blocks, width = activations.shape
    count = 2 * blocks
    tok, grp, out = (lax.axis_size(name) for name in ("tok", "grp", "out"))
    block = width * out
    token_count = tok_dev * tok * grp
    part = width // grp
    local_sides = jnp.concatenate([activations, out_grads], axis=1)
    pieces = jnp.swapaxes(local_sides, 0, 1)
    mine = lax.all_to_all(pieces, "tok", split_axis=0, concat_axis=0, tiled=True)
    mine = mine.reshape(tok * tok_dev, width)
    whole = lax.all_gather(mine, ("grp", "out"), axis=0, tiled=False)
    whole = whole.reshape(grp, out, tok * tok_dev, width)
    sides = jnp.transpose(whole, (0, 2, 1, 3)).reshape(token_count, block)
    start = lax.axis_index("out") * width + lax.axis_index("grp") * part
    cols = lax.dynamic_slice_in_dim(sides, start, part, 1)
    whitened = token_space_whiten(sides, cols)
    spread_low = lax.all_gather(whitened, ("tok", "grp"), axis=0, tiled=False)
    spread_low = spread_low.reshape(count, grp, token_count, part)
    grads_low = spread_low[blocks:]
    row = lax.axis_index(("tok", "grp"))
    own = lax.dynamic_index_in_dim(spread_low, row // out, 0, keepdims=False)
    owner = lax.rem(row, out) == lax.axis_index("out")
    acts_low = lax.psum(jnp.where(owner, own, jnp.zeros_like(own)), "out")
    update = jnp.einsum("yta,bxtc->yabxc", acts_low, grads_low, preferred_element_type=jnp.float32)
    update = (update / math.sqrt(token_count)).astype(jnp.bfloat16).reshape(width, blocks, width)
    grads_whole = spread(out_grads)
    weight_rows = weight.reshape(blocks, width, blocks, block)
    input_grad = jnp.einsum(
        "tjq,bcjq->tbc", grads_whole, weight_rows, preferred_element_type=jnp.float32
    ).astype(jnp.bfloat16)
    return (update, input_grad)


def solution(mesh):
    in_specs = (
        P(("tok", "grp"), None, "out"),
        P(("tok", "grp"), None, "out"),
        P(None, "out", None),
    )
    out_specs = (P(("tok", "grp"), None, "out"), P(("tok", "grp"), None, "out"))

    def body(activations, out_grads, weight):
        blocks = activations.shape[1]
        tok, grp, out = (mesh.shape[name] for name in ("tok", "grp", "out"))
        fits = tok == 2 * blocks and tok * grp == blocks * out
        return (planes if fits else local)(activations, out_grads, weight)

    return jax.shard_map(body, mesh=mesh, in_specs=in_specs, out_specs=out_specs, check_vma=False)
```

profile of v0, /device:TPU:0, one launch (start us, length us, event | category | flops | bytes accessed | tf_op | source)
XLA Modules:
  0.0 237.2 jit_solution(17187461038520449811)
XLA Ops:
  7.2 1.0 copy.28
  8.2 1.1 copy.27
  9.3 20.7 %all_to_all.5 = bf16[4,128,512]{2,1,0:T(8,128)(2,1)} all-to-all(bf16[4,128,512]{2,1,0:T(8,128)(2,1)S(1)} %maximum_bitcast_fusion), channel_id=1, replica_groups=mesh['tok'=4,'out'=4,'grp'=2] {'tok'}, dimensions={0} | all-to-all | bytes 1048576 | tf_op jit(solution)/shard_map/all_to_all | solution.py:158
  30.2 35.8 %all-gather.5.cloned.1.call-done = bf16[8,512,512]{2,1,0:T(8,128)(2,1)} async-done(((bf16[1,512,512]{2,1,0:T(8,128)(2,1)}), bf16[8,512,512]{2,1,0:T(8,128)(2,1)}) %all-gather.5.cloned.1.call-update) | async-done | bytes 4194320 | tf_op jit(solution)/shard_map/all_gather | solution.py:160
  66.0 3.0 %convert_reduce_fusion = f32[2,512]{1,0:T(2,128)S(1)} fusion(bf16[2,512,4,512]{3,1,2,0:T(8,128)(2,1)} %bitcast.45), kind=kLoop, calls=%fused_computation.3 | loop fusion | flops 4193280 | bytes 4198400 | tf_op jit(solution)/shard_map/reduce_sum | solution.py:114
  69.4 3.2 %copy.29 = bf16[2,512,4,512]{3,2,1,0:T(4,128)(2,1)S(1)} copy(bf16[2,512,4,512]{3,1,2,0:T(8,128)(2,1)S(1)} %bitcast.46) | data formatting | bytes 8388608 | tf_op jit(solution)/shard_map/transpose | solution.py:162
  73.3 1.4 copy.42
  74.7 4.5 %multiply_reduce_fusion.1 = (f32[1024]{0:T(1024)S(1)}, f32[1024,1024]{0,1:T(8,128)S(1)}) fusion(f32[1024]{0:T(1024)S(1)} %broadcast_multiply_fusion.1, bf16[1024,2048]{1,0:T(8,128)(2,1)S(1)} %bitcast.48), kind=kOutput, calls=%fused_computation.6 | convolution fusion | flops 4297063424 | bytes 8396800 | tf_op jit(solution)/shard_map/tc,uc->tu/dot_general | solution.py:113
  79.3 1.9 copy-done
  87.7 2.8 %divide_convert_fusion = bf16[1024,1024]{0,1:T(8,128)(2,1)S(1)} fusion(f32[1024,1024]{0,1:T(8,128)} %copy-done, f32[]{:T(128)S(6)} %div.88), kind=kLoop, calls=%fused_computation.4 | loop fusion | flops 3145728 | bytes 6291460 | tf_op jit(solution)/shard_map/convert_element_type | solution.py:132
  90.6 2.1 fusion.8
  92.8 0.8 convolution_add_fusion.2
  93.6 0.9 fusion.7
  94.5 1.8 fusion.10
  97.1 72.0 %all-gather.9.cloned.1.call-done = bf16[8192,256]{1,0:T(8,128)(2,1)} async-done(((bf16[1024,256]{1,0:T(8,128)(2,1)}), bf16[8192,256]{1,0:T(8,128)(2,1)}) %all-gather.9.cloned.1.call-update) | async-done | bytes 4194320 | tf_op jit(solution)/shard_map/all_gather | solution.py:166
  169.1 1.3 constant_dynamic-slice_fusion
  170.9 1.0 select_bitcast_fusion
  172.0 14.5 %all-gather.7.cloned.1.call-done = bf16[128,2,2048]{2,0,1:T(8,128)(2,1)} async-done(((bf16[128,2,512]{2,0,1:T(8,128)(2,1)}), bf16[128,2,2048]{2,0,1:T(8,128)(2,1)}) %all-gather.7.cloned.1.call-update) | async-done | bytes 1048592 | tf_op jit(solution)/shard_map/all_gather | solution.py:13
  186.5 6.7 %fusion.14 = bf16[128,2,512]{2,0,1:T(8,128)(2,1)S(1)} fusion(bf16[2,64,2,8,2048]{4,3,2,1,0:T(8,128)(2,1)} %bitcast.57, bf16[128,2,2048]{2,0,1:T(8,128)(2,1)} %all-gather.7.cloned.1.call-done), kind=kOutput, calls=%fused_computation.23 | convolution fusion | flops 1073872896 | bytes 9699328 | tf_op jit(solution)/shard_map/tjq,bcjq->tbc/dot_general | solution.py:177
  193.3 1.0 copy.35
  194.4 31.2 %all-reduce.2.cloned.1.call-done = bf16[2,1024,256]{1,2,0:T(8,128)(2,1)} async-done(((bf16[2,1024,256]{1,2,0:T(8,128)(2,1)}), bf16[2,1024,256]{1,2,0:T(8,128)(2,1)}) %all-reduce.2.cloned.1.call-update) | async-done | bytes 1048592 | tf_op jit(solution)/shard_map/psum | solution.py:172
  225.6 2.5 %multiply_convert_fusion = bf16[2,256,2,2,256]{4,1,3,2,0:T(8,128)(2,1)S(1)} fusion(bf16[2,2,1024,256,1]{3,2,1,0,4:T(8,128)(2,1)S(1)} %bitcast.51, bf16[2,1024,256]{1,2,0:T(8,128)(2,1)} %all-reduce.2.cloned.1.call-done), kind=kOutput, calls=%fused_computation.7 | convolution fusion | flops 1074790400 | bytes 4194304 | tf_op jit(solution)/shard_map/yta,bxtc->yabxc/dot_general | solution.py:173
  228.1 1.1 copy.38
  229.2 1.5 reshape.68
  (26 shorter events, 3.7 us)
Async XLA Ops:
  7.2 58.8 %all-gather.5.cloned.1.call-start = ((), (), s32[]{:S(2)}) async-start(), calls=%async_computation.1 | async-start | bytes 4718592 | tf_op jit(solution)/shard_map/all_gather | solution.py:160
  8.2 64.5 %copy-start.4 = (bf16[128,2,512]{2,0,1:T(8,128)(2,1)}, bf16[128,2,512]{2,0,1:T(8,128)(2,1)S(1)}, u32[]{:S(2)}) copy-start(bf16[128,2,512]{2,0,1:T(8,128)(2,1)S(1)} %copy.28) | copy-start | bytes 786436
  30.1 139.0 %all-gather.9.cloned.1.call-start = ((), (), s32[]{:S(2)}) async-start(), calls=%async_computation.4 | async-start | bytes 4718592 | tf_op jit(solution)/shard_map/all_gather | solution.py:166
  66.0 3.4 %copy-start.1 = (bf16[8,512,512]{2,1,0:T(8,128)(2,1)S(1)}, bf16[8,512,512]{2,1,0:T(8,128)(2,1)}, u32[]{:S(2)}) copy-start(bf16[8,512,512]{2,1,0:T(8,128)(2,1)} %all-gather.5.cloned.1.call-done) | copy-start | bytes 12582916
  74.7 4.6 %copy-start.2 = (bf16[128,8,4,512]{3,1,2,0:T(8,128)(2,1)}, bf16[128,8,4,512]{3,1,2,0:T(8,128)(2,1)S(1)}, u32[]{:S(2)}) copy-start(bf16[128,8,4,512]{3,1,2,0:T(8,128)(2,1)S(1)} %copy.42) | copy-start | bytes 12582916
  79.2 2.0 copy-start
  96.3 90.2 %all-gather.7.cloned.1.call-start = ((), (), s32[]{:S(2)}) async-start(), calls=%async_computation.3 | async-start | bytes 1310720 | tf_op jit(solution)/shard_map/all_gather | solution.py:13
  97.1 128.6 %all-reduce.2.cloned.1.call-start = ((), (), s32[]{:S(2)}) async-start(), calls=%async_computation.2 | async-start | bytes 2097152 | tf_op jit(solution)/shard_map/psum | solution.py:172
  186.5 7.7 %copy-start.3 = (bf16[8192,256]{1,0:T(8,128)(2,1)S(1)}, bf16[8192,256]{1,0:T(8,128)(2,1)}, u32[]{:S(2)}) copy-start(bf16[8192,256]{1,0:T(8,128)(2,1)} %all-gather.9.cloned.1.call-done) | copy-start | bytes 12582916
Sparse Core Ops, SparseCore 0:
  30.2 35.6 all-gather.4
  96.4 72.6 all-gather.8
  171.2 15.2 all-gather.6
  189.3 36.2 all-reduce.1
where the time goes:
time: 238 us; the launch traced here: 237 us
  waiting for transfers between devices  154 us (65%)
  blocking collectives  20.7 us (9%)
  between operations  19.6 us (8%)
  matrix products  19.4 us (8%)
  local copies, waits for them, and re-layouts  14.6 us (6%)
  other arithmetic  8.42 us (4%)
    all_gather x1, waiting for transfers between devices, planes(): spread_low = lax.all_gather(whitened, ('tok', 'grp'), axis=0, tiled=False)  72 us
    all_gather x1, waiting for transfers between devices, planes(): whole = lax.all_gather(mine, ('grp', 'out'), axis=0, tiled=False)  35.8 us
    psum x1, waiting for transfers between devices, planes(): acts_low = lax.psum(jnp.where(owner, own, jnp.zeros_like(own)), 'out')  31.2 us
    all_to_all x1, blocking collectives, planes(): lax.all_to_all(pieces, 'tok', split_axis=0, concat_axis=0, tiled=True)  20.7 us
    all_gather x1, waiting for transfers between devices, spread(): return lax.all_gather(piece, 'out', axis=2, tiled=True)  14.5 us
    unnamed x18, local copies, waits for them, and re-layouts  9.98 us
    dot_general x1, matrix products, planes(): jnp.einsum('tjq,bcjq->tbc', grads_whole, weight_rows, preferred_element_t...  6.75 us
    dot_general x4, matrix products, apply(): jnp.einsum('tu,uc->tc', low, value.astype(jnp.bfloat16), preferred_elemen...  5.66 us
  transfers between devices with their start and end apart: 4, of which 4 were waited for; matrix products, arithmetic and copies ran while one was open for 5% of the time, Pallas kernels for 0%

commit v1 on v0

--- a/solution.py
+++ b/solution.py
@@ -10,7 +10,7 @@
 
 
 def spread(piece):
-    return lax.all_gather(piece, "out", axis=2, tiled=True)
+    return jnp.concatenate(lax.all_gather(piece, "out"), axis=2)
 
 
 def token_sums(maker, rows):

time: 238 us -> 219 us (0.920)
  waiting for transfers between devices: 154 us -> 133 us
  local copies, waits for them, and re-layouts: 14.6 us -> 17.4 us
    all_gather x1, waiting for transfers between devices: 14.5 us -> 0.02 us  [spread(): return jnp.concatenate(lax.all_gather(piece, 'out'), axis=2)]
    psum x1, waiting for transfers between devices: 31.2 us -> 27.4 us  [planes(): acts_low = lax.psum(jnp.where(owner, own, jnp.zeros_like(own)), 'out')]
    unnamed x18 -> x16, local copies, waits for them, and re-layouts: 9.98 us -> 9.88 us
  transfers between devices with their start and end apart: 4 -> 4, of which waited for: 4 -> 3; matrix products, arithmetic and copies ran while one was open for 5% -> 15% of each run, Pallas kernels for 0% -> 0%
where the time goes in v1:
time: 219 us
  waiting for transfers between devices  133 us (61%)
  blocking collectives  20.7 us (9%)
  between operations  19.9 us (9%)
  matrix products  19.1 us (9%)
  local copies, waits for them, and re-layouts  17.4 us (8%)
  other arithmetic  8.48 us (4%)
    all_gather x1, waiting for transfers between devices, planes(): spread_low = lax.all_gather(whitened, ('tok', 'grp'), axis=0, tiled=False)  69.8 us
    all_gather x1, waiting for transfers between devices, planes(): whole = lax.all_gather(mine, ('grp', 'out'), axis=0, tiled=False)  35 us
    psum x1, waiting for transfers between devices, planes(): acts_low = lax.psum(jnp.where(owner, own, jnp.zeros_like(own)), 'out')  27.4 us
    all_to_all x1, blocking collectives, planes(): lax.all_to_all(pieces, 'tok', split_axis=0, concat_axis=0, tiled=True)  20.7 us
    unnamed x16, local copies, waits for them, and re-layouts  9.88 us
    dot_general x1, matrix products, planes(): jnp.einsum('tjq,bcjq->tbc', grads_whole, weight_rows, preferred_element_t...  6.41 us
    dot_general x4, matrix products, apply(): jnp.einsum('tu,uc->tc', low, value.astype(jnp.bfloat16), preferred_elemen...  5.66 us
    dot_general x1, matrix products, token_space_whiten(): jnp.einsum('tc,uc->tu', sides, sides, preferred_element_type=jnp.float32)  4.53 us
  transfers between devices with their start and end apart: 4, of which 3 were waited for; matrix products, arithmetic and copies ran while one was open for 15% of the time, Pallas kernels for 0%

profile of v1, /device:TPU:0, one launch (start us, length us, event | category | flops | bytes accessed | tf_op | source)
XLA Modules:
  0.0 218.8 jit_solution(11139871494118409330)
XLA Ops:
  7.2 1.0 copy.27
  8.2 1.0 copy.28
  9.2 20.7 %all_to_all.5 = bf16[4,128,512]{2,1,0:T(8,128)(2,1)} all-to-all(bf16[4,128,512]{2,1,0:T(8,128)(2,1)S(1)} %maximum_bitcast_fusion), channel_id=1, replica_groups=mesh['tok'=4,'out'=4,'grp'=2] {'tok'}, dimensions={0} | all-to-all | bytes 1048576 | tf_op jit(solution)/shard_map/all_to_all | solution.py:158
  30.8 35.0 %all-gather.6.cloned.1.call-done = bf16[8,512,512]{2,1,0:T(8,128)(2,1)} async-done(((bf16[1,512,512]{2,1,0:T(8,128)(2,1)}), bf16[8,512,512]{2,1,0:T(8,128)(2,1)}) %all-gather.6.cloned.1.call-update) | async-done | bytes 4194320 | tf_op jit(solution)/shard_map/all_gather | solution.py:160
  65.8 3.0 %convert_reduce_fusion = f32[2,512]{1,0:T(2,128)S(1)} fusion(bf16[2,512,4,512]{3,1,2,0:T(8,128)(2,1)} %bitcast.49), kind=kLoop, calls=%fused_computation.3 | loop fusion | flops 4193280 | bytes 4198400 | tf_op jit(solution)/shard_map/reduce_sum | solution.py:114
  69.3 3.2 %copy.29 = bf16[2,512,4,512]{3,2,1,0:T(4,128)(2,1)S(1)} copy(bf16[2,512,4,512]{3,1,2,0:T(8,128)(2,1)S(1)} %bitcast.50) | data formatting | bytes 8388608 | tf_op jit(solution)/shard_map/transpose | solution.py:162
  73.1 1.4 copy.42
  74.6 4.5 %multiply_reduce_fusion.1 = (f32[1024]{0:T(1024)S(1)}, f32[1024,1024]{0,1:T(8,128)S(1)}) fusion(f32[1024]{0:T(1024)S(1)} %broadcast_multiply_fusion.1, bf16[1024,2048]{1,0:T(8,128)(2,1)S(1)} %bitcast.52), kind=kOutput, calls=%fused_computation.6 | convolution fusion | flops 4297063424 | bytes 8396800 | tf_op jit(solution)/shard_map/tc,uc->tu/dot_general | solution.py:113
  79.1 1.9 copy-done
  88.0 2.8 %divide_convert_fusion = bf16[1024,1024]{0,1:T(8,128)(2,1)S(1)} fusion(f32[1024,1024]{0,1:T(8,128)} %copy-done, f32[]{:T(128)S(6)} %div.88), kind=kLoop, calls=%fused_computation.4 | loop fusion | flops 3145728 | bytes 6291460 | tf_op jit(solution)/shard_map/convert_element_type | solution.py:132
  90.9 2.1 fusion.8
  93.8 0.9 fusion.7
  94.7 1.8 fusion.10
  96.7 2.0 copy.53
  98.7 0.8 reshape.75
  99.5 69.8 %all-gather.8.cloned.1.call-done = bf16[8192,256]{1,0:T(8,128)(2,1)} async-done(((bf16[1024,256]{1,0:T(8,128)(2,1)}), bf16[8192,256]{1,0:T(8,128)(2,1)}) %all-gather.8.cloned.1.call-update) | async-done | bytes 4194320 | tf_op jit(solution)/shard_map/all_gather | solution.py:166
  169.4 1.3 constant_dynamic-slice_fusion
  171.2 1.0 select_bitcast_fusion
  172.3 6.4 %fusion.14 = bf16[128,2,512]{2,0,1:T(8,128)(2,1)S(1)} fusion(bf16[128,2,2048,1]{2,0,1,3:T(8,128)(2,1)S(1)} %reshape.75, bf16[2,64,2,8,2048]{4,3,2,1,0:T(8,128)(2,1)} %bitcast.63), kind=kOutput, calls=%fused_computation.23 | convolution fusion | flops 1073872896 | bytes 9699328 | tf_op jit(solution)/shard_map/tjq,bcjq->tbc/dot_general | solution.py:177
  178.7 1.0 copy.35
  179.8 27.4 %all-reduce.2.cloned.1.call-done = bf16[2,1024,256]{1,2,0:T(8,128)(2,1)} async-done(((bf16[2,1024,256]{1,2,0:T(8,128)(2,1)}), bf16[2,1024,256]{1,2,0:T(8,128)(2,1)}) %all-reduce.2.cloned.1.call-update) | async-done | bytes 1048592 | tf_op jit(solution)/shard_map/psum | solution.py:172
  207.2 2.5 %multiply_convert_fusion = bf16[2,256,2,2,256]{4,1,3,2,0:T(8,128)(2,1)S(1)} fusion(bf16[2,2,1024,256,1]{3,2,1,0,4:T(8,128)(2,1)S(1)} %bitcast.56, bf16[2,1024,256]{1,2,0:T(8,128)(2,1)} %all-reduce.2.cloned.1.call-done), kind=kOutput, calls=%fused_computation.7 | convolution fusion | flops 1074790400 | bytes 4194304 | tf_op jit(solution)/shard_map/yta,bxtc->yabxc/dot_general | solution.py:173
  209.7 1.1 copy.38
  210.8 1.5 reshape.77
  (26 shorter events, 4.6 us)
Async XLA Ops:
  7.2 58.7 %all-gather.6.cloned.1.call-start = ((), (), s32[]{:S(2)}) async-start(), calls=%async_computation.1 | async-start | bytes 4718592 | tf_op jit(solution)/shard_map/all_gather | solution.py:160
  30.0 66.7 %all-gather.10.cloned.1.call-start = ((), (), s32[]{:S(2)}) async-start(), calls=%async_computation.4 | async-start | bytes 1310720 | tf_op jit(solution)/shard_map/all_gather | solution.py:13
  30.8 138.6 %all-gather.8.cloned.1.call-start = ((), (), s32[]{:S(2)}) async-start(), calls=%async_computation.3 | async-start | bytes 4718592 | tf_op jit(solution)/shard_map/all_gather | solution.py:166
  65.8 3.4 %copy-start.1 = (bf16[8,512,512]{2,1,0:T(8,128)(2,1)S(1)}, bf16[8,512,512]{2,1,0:T(8,128)(2,1)}, u32[]{:S(2)}) copy-start(bf16[8,512,512]{2,1,0:T(8,128)(2,1)} %all-gather.6.cloned.1.call-done) | copy-start | bytes 12582916
  74.5 4.6 %copy-start.2 = (bf16[128,8,4,512]{3,1,2,0:T(8,128)(2,1)}, bf16[128,8,4,512]{3,1,2,0:T(8,128)(2,1)S(1)}, u32[]{:S(2)}) copy-start(bf16[128,8,4,512]{3,1,2,0:T(8,128)(2,1)S(1)} %copy.42) | copy-start | bytes 12582916
  79.1 2.0 copy-start
  96.6 110.6 %all-reduce.2.cloned.1.call-start = ((), (), s32[]{:S(2)}) async-start(), calls=%async_computation.2 | async-start | bytes 2097152 | tf_op jit(solution)/shard_map/psum | solution.py:172
  172.3 7.4 %copy-start.3 = (bf16[8192,256]{1,0:T(8,128)(2,1)S(1)}, bf16[8192,256]{1,0:T(8,128)(2,1)}, u32[]{:S(2)}) copy-start(bf16[8192,256]{1,0:T(8,128)(2,1)} %all-gather.8.cloned.1.call-done) | copy-start | bytes 12582916
Sparse Core Ops, SparseCore 0:
  30.1 35.6 all-gather.5
  67.4 16.7 all-gather.9
  96.7 72.6 all-gather.7
  172.4 34.7 all-reduce.1
